TPU v7x, 256 devices: a whole 4x4x8 slice. The times are simulated.
256 devices in a mesh: lat: 64 (over y, x, z_hi), scale: 4 (over z_lo, core).
Axes of the slice: x: 4, y: 4, z: 8 (z_hi: 4, z_lo: 2; z = z_hi * 2 + z_lo), core: 2. Of those that a mesh axis runs over, the one named last changes fastest.
Arguments:
- state: float32 [512, 2, 128, 512], P('lat', None, None, 'scale'), may hold values from -6 to 6
- noise: float32 [512, 2, 128, 512], P('lat', None, None, 'scale'), may hold values from -6 to 6
- slot_wavenumber: int32 [512], replicated, may hold values from 0 to 511, each once
- timescale: float32 [128], replicated, may hold values from 2 to 50
- lengthscale: float32 [128], replicated, may hold values from 128 to 512
Outputs:
- new_state: float32 [512, 2, 128, 512], P('lat', None, None, 'scale')
- pattern: float32 [128, 1536, 3072], P('scale', 'lat')
Inputs may be any that keep to these rules, and one draw needn't show every extreme that they name: `slot_wavenumber`: each wavenumber 0 to 511 stands in exactly one slot.
All inputs are finite; a program needn't handle non-finite values.
Results may differ from a plain program's by a relative error of at most 0.0069.
Values may be sent and summed in bfloat16 or wider, within the bound.
No kernel may reach another device: no remote copies, remote signals or barrier semaphores. Data moves between devices by JAX's collectives and lax.ppermute only.
A program may use at most 192 MiB of HBM per device.

v0:
```python
import math

import jax
import jax.numpy as jnp
import numpy as np
from jax import lax
from jax.experimental import pallas as pl
from jax.experimental.pallas import tpu as pltpu
from jax.sharding import PartitionSpec as P

M = 512
NLAT = 1536
NLON = 3072
FIELDS = 128
HALF = NLAT // 2
LANES = 128
LAT_PARTS = 64
SCALE_PARTS = 4
SLOTS = M // LAT_PARTS
ROWS = NLAT // LAT_PARTS
OWN_FIELDS = FIELDS // SCALE_PARTS
PAIRS = SLOTS // 2
CHUNK = 128
WIDTH = 512

log_floor = -60.0


def vmem_params(*semantics):
    return pltpu.CompilerParams(
        dimension_semantics=semantics, vmem_limit_bytes=56 * 1024 * 1024
    )


def latitude_constants():
    colatitude = (np.arange(HALF) + 0.5) * (math.pi / NLAT)
    cosine = np.cos(colatitude)
    log_sine = np.log(np.sin(colatitude))
    return np.stack([cosine, log_sine]).astype(np.float32)


def log_head_table():
    lgamma = np.vectorize(math.lgamma)
    order = np.arange(M, dtype=np.float64)
    head = (
        0.5 * (lgamma(2.0 * order + 1.0) + np.log(2.0 * order + 1.0) - math.log(2.0))
        - order * math.log(2.0)
        - lgamma(order + 1.0)
    )
    return head.astype(np.float32)[None]


def update_kernel(where_ref, scales_ref, state_ref, noise_ref, new_ref, spectra_ref, factor):
    @pl.when(pl.program_id(0) == 0)
    def _():
        time_row = jnp.broadcast_to(scales_ref[0:1, :], (FIELDS, FIELDS))
        length_row = jnp.broadcast_to(scales_ref[1:2, :], (FIELDS, FIELDS))
        timescale = time_row.T
        lengthscale = length_row.T
        decay = jnp.exp(-1.0 / timescale)
        first = where_ref[1] * CHUNK
        degree = (first + lax.broadcasted_iota(jnp.int32, (FIELDS, CHUNK), 1)).astype(jnp.float32)
        factor[0] = decay
        factor[1] = (
            jnp.sqrt(1.0 - decay * decay)
            * jnp.exp(-degree * (degree + 1.0) / (2.0 * (lengthscale * lengthscale)))
            * (M / lengthscale)
        )

    for part in range(2):
        new = factor[0] * state_ref[0, part] + factor[1] * noise_ref[0, part]
        new_ref[0, part] = new
        rounded = new.astype(jnp.bfloat16)
        for owner in range(SCALE_PARTS):
            spectra_ref[owner, 0, part] = rounded[owner * OWN_FIELDS : (owner + 1) * OWN_FIELDS]


def update(where, scales, state, noise):
    block = pl.BlockSpec((1, 2, FIELDS, CHUNK), lambda s: (s, 0, 0, 0))
    return pl.pallas_call(
        update_kernel,
        grid=(SLOTS,),
        in_specs=[
            pl.BlockSpec(memory_space=pltpu.SMEM),
            pl.BlockSpec((2, FIELDS), lambda s: (0, 0)),
            block,
            block,
        ],
        out_specs=[
            block,
            pl.BlockSpec((SCALE_PARTS, 1, 2, OWN_FIELDS, CHUNK), lambda s: (0, s, 0, 0, 0)),
        ],
        out_shape=[
            jax.ShapeDtypeStruct((SLOTS, 2, FIELDS, CHUNK), jnp.float32),
            jax.ShapeDtypeStruct((SCALE_PARTS, SLOTS, 2, OWN_FIELDS, CHUNK), jnp.bfloat16),
        ],
        scratch_shapes=[pltpu.VMEM((2, FIELDS, CHUNK), jnp.float32)],
        compiler_params=vmem_params("arbitrary"),
        name="update",
    )(where, scales, state, noise)


def own_orders(where_ref, orders_ref, shape):
    slot = lax.broadcasted_iota(jnp.int32, shape, 0)
    orders = jnp.zeros(shape, jnp.int32)
    for s in range(SLOTS):
        orders = jnp.where(slot == s, orders_ref[where_ref[0] * SLOTS + s], orders)
    return orders


def ratio_at(degree, orders):
    squared = degree * degree
    return jnp.sqrt(jnp.maximum(squared - orders * orders, 0.0) / (4.0 * squared - 1.0))


def table_kernel(where_ref, orders_ref, lats_ref, head_ref, table_ref, rows, carried, pole):
    step = pl.program_id(0)
    order_tile = own_orders(where_ref, orders_ref, (SLOTS, LANES))
    order_real = order_tile.astype(jnp.float32)

    @pl.when(step == 0)
    def _():
        wide = own_orders(where_ref, orders_ref, (SLOTS, M))
        chosen = lax.broadcasted_iota(jnp.int32, (SLOTS, M), 1) == wide
        head = jnp.sum(jnp.where(chosen, head_ref[...], 0.0), axis=1, keepdims=True)
        log_start = head + order_real[:, :1] * lats_ref[1:2, :]
        pole[...] = jnp.where(
            log_start >= log_floor, jnp.exp(jnp.maximum(log_start, log_floor)), 0.0
        )
        carried[...] = jnp.zeros_like(carried)

    degree = (step * CHUNK + lax.broadcasted_iota(jnp.int32, (SLOTS, LANES), 1)).astype(jnp.float32)
    above = degree > order_real
    here = jnp.where(above, ratio_at(degree, order_real), 1.0)
    gain = jnp.where(above, 1.0 / here, 0.0)
    loss = jnp.where(above, ratio_at(degree - 1.0, order_real) / here, 0.0)
    cosine = jnp.broadcast_to(lats_ref[0:1, :], (SLOTS, HALF))
    start = pole[...]
    previous = carried[0]
    earlier = carried[1]
    for i in range(CHUNK):
        begins = order_tile[:, :1] == step * CHUNK + i
        new = gain[:, i : i + 1] * (cosine * previous) - loss[:, i : i + 1] * earlier
        new = jnp.where(begins, start, new)
        for tile in range(HALF // LANES):
            rows[tile, i * SLOTS : (i + 1) * SLOTS, :] = new[:, tile * LANES : (tile + 1) * LANES]
        previous, earlier = (new, previous)
    carried[0] = previous
    carried[1] = earlier
    for s in range(SLOTS):
        for tile in range(HALF // LANES):
            table_ref[s, :, tile * LANES : (tile + 1) * LANES] = rows[
                tile, pl.ds(s, CHUNK, stride=SLOTS), :
            ].astype(jnp.bfloat16)


def legendre_table(where, orders, lats, head):
    return pl.pallas_call(
        table_kernel,
        grid=(M // CHUNK,),
        in_specs=[
            pl.BlockSpec(memory_space=pltpu.SMEM),
            pl.BlockSpec(memory_space=pltpu.SMEM),
            pl.BlockSpec((2, HALF), lambda i: (0, 0)),
            pl.BlockSpec((1, M), lambda i: (0, 0)),
        ],
        out_specs=pl.BlockSpec((SLOTS, CHUNK, HALF), lambda i: (0, i, 0)),
        out_shape=jax.ShapeDtypeStruct((SLOTS, M, HALF), jnp.bfloat16),
        scratch_shapes=[
            pltpu.VMEM((HALF // LANES, CHUNK * SLOTS, LANES), jnp.float32),
            pltpu.VMEM((2, SLOTS, HALF), jnp.float32),
            pltpu.VMEM((SLOTS, HALF), jnp.float32),
        ],
        compiler_params=vmem_params("arbitrary"),
        name="legendre",
    )(where, orders, lats, head)


def project_kernel(where_ref, orders_ref, spectra_ref, table_ref, out_ref):
    pair = pl.program_id(0)
    north = []
    south = []
    lane = lax.broadcasted_iota(jnp.int32, (1, CHUNK), 1)
    for half in range(2):
        order = orders_ref[where_ref[0] * SLOTS + 2 * pair + half]
        sign = (1 - 2 * ((lane + order) % 2)).astype(jnp.float32).astype(jnp.bfloat16)
        blocks = [
            spectra_ref[b, half].reshape(2 * OWN_FIELDS, CHUNK) for b in range(SCALE_PARTS)
        ]
        left = jnp.concatenate(
            [jnp.concatenate([b, b * sign], axis=0) for b in blocks], axis=1
        )
        product = jnp.dot(left, table_ref[half], preferred_element_type=jnp.float32)
        north.append(product[: 2 * OWN_FIELDS])
        south.append(product[2 * OWN_FIELDS :])
    upper = jnp.concatenate(north, axis=0).T.reshape(LAT_PARTS // 2, ROWS, LANES)
    lower = jnp.concatenate(south, axis=0).T.reshape(LAT_PARTS // 2, ROWS, LANES)
    upper = upper.astype(jnp.bfloat16)
    lower = lower.astype(jnp.bfloat16)
    for d in range(LAT_PARTS // 2):
        out_ref[d, 0] = upper[d]
        out_ref[LAT_PARTS - 1 - d, 0] = lower[d]


def project(where, orders, spectra, table):
    return pl.pallas_call(
        project_kernel,
        grid=(PAIRS,),
        in_specs=[
            pl.BlockSpec(memory_space=pltpu.SMEM),
            pl.BlockSpec(memory_space=pltpu.SMEM),
            pl.BlockSpec(
                (SCALE_PARTS, 2, 2, OWN_FIELDS, CHUNK), lambda p: (0, p, 0, 0, 0)
            ),
            pl.BlockSpec((2, M, HALF), lambda p: (p, 0, 0)),
        ],
        out_specs=pl.BlockSpec((LAT_PARTS, 1, ROWS, LANES), lambda p: (0, p, 0, 0)),
        out_shape=jax.ShapeDtypeStruct((LAT_PARTS, PAIRS, ROWS, LANES), jnp.bfloat16),
        compiler_params=vmem_params("arbitrary"),
        name="project",
    )(where, orders, spectra, table)


def fourier_table(slot_wavenumber):
    orders = slot_wavenumber.reshape(LAT_PARTS, 2, 2, 2).transpose(1, 3, 2, 0)
    orders = orders.reshape(2, 2, 1, 2 * LAT_PARTS)
    orders = jnp.broadcast_to(orders, (2, 2, 2, 2 * LAT_PARTS)).reshape(2 * M, 1)
    row = lax.broadcasted_iota(jnp.int32, (2 * M, 1), 0)
    quarter = (row // (2 * LAT_PARTS)) % 2 * (NLON // 4)
    points = lax.broadcasted_iota(jnp.int32, (1, NLON), 1)
    phase_index = (orders * points + quarter) % NLON
    angles = phase_index.astype(jnp.float32) * (2.0 * math.pi / NLON)
    weight = jnp.where(orders == 0, 1.0, 2.0) / M
    return (weight * jnp.cos(angles)).astype(jnp.bfloat16)


def synthesis_kernel(where_ref, grid_ref, fourier_ref, out_ref, wide, turned, left):
    @pl.when(pl.program_id(0) == 0)
    def _():
        wide[...] = grid_ref[...].astype(jnp.float32).reshape(wide.shape)
        is_south = where_ref[0] >= LAT_PARTS // 2
        for row in range(ROWS):
            target = jnp.where(is_south, ROWS - 1 - row, row)
            for group in range(2):
                stacked = jnp.concatenate(
                    [
                        wide[pl.ds((2 * group + t) * ROWS + row, LAT_PARTS, stride=PAIRS * ROWS), :]
                        for t in range(2)
                    ],
                    axis=0,
                ).T
                for q in range(4):
                    turned[4 * group + q, pl.ds(target, OWN_FIELDS, stride=ROWS), :] = stacked[
                        q * OWN_FIELDS : (q + 1) * OWN_FIELDS
                    ]
        for q in range(8):
            left[:, q * LANES : (q + 1) * LANES] = turned[q].astype(jnp.bfloat16)

    product = jnp.dot(left[...], fourier_ref[...], preferred_element_type=jnp.float32)
    out_ref[...] = product.reshape(out_ref.shape)


def synthesize(where, grid_spec, fourier):
    return pl.pallas_call(
        synthesis_kernel,
        grid=(NLON // WIDTH,),
        in_specs=[
            pl.BlockSpec(memory_space=pltpu.SMEM),
            pl.BlockSpec((LAT_PARTS, PAIRS, ROWS, LANES), lambda k: (0, 0, 0, 0)),
            pl.BlockSpec((2 * M, WIDTH), lambda k: (0, k)),
        ],
        out_specs=pl.BlockSpec((OWN_FIELDS, ROWS, WIDTH), lambda k: (0, 0, k)),
        out_shape=jax.ShapeDtypeStruct((OWN_FIELDS, ROWS, NLON), jnp.float32),
        scratch_shapes=[
            pltpu.VMEM((LAT_PARTS * PAIRS * ROWS, LANES), jnp.float32),
            pltpu.VMEM((8, OWN_FIELDS * ROWS, LANES), jnp.float32),
            pltpu.VMEM((OWN_FIELDS * ROWS, 2 * M), jnp.bfloat16),
        ],
        compiler_params=vmem_params("arbitrary"),
        name="synthesis",
    )(where, grid_spec, fourier)


def exchanged(spectra):
    return lax.all_to_all(spectra, "scale", 0, 0, tiled=True)


def on_device(state, noise, slot_wavenumber, timescale, lengthscale):
    where = jnp.stack([lax.axis_index("lat"), lax.axis_index("scale")])
    scales = jnp.stack([timescale, lengthscale])
    lats = jnp.asarray(latitude_constants())
    head = jnp.asarray(log_head_table())
    new_state, spectra = update(where, scales, state, noise)
    spectra = exchanged(spectra)
    table = legendre_table(where, slot_wavenumber, lats, head)
    grid_spec = project(where, slot_wavenumber, spectra, table)
    grid_spec = lax.all_to_all(grid_spec, "lat", 0, 0, tiled=True)
    pattern = synthesize(where, grid_spec, fourier_table(slot_wavenumber))
    return (new_state, pattern)


def solution(mesh):
    placed = (P("lat", None, None, "scale"), P("lat", None, None, "scale"), P(), P(), P())
    return jax.shard_map(
        on_device,
        mesh=mesh,
        in_specs=placed,
        out_specs=(P("lat", None, None, "scale"), P("scale", "lat", None)),
        check_vma=False,
    )
```

profile of v0, /device:TPU:1, one launch (start us, length us, event | category | flops | bytes accessed | tf_op | source)
XLA Modules:
  0.0 108.6 jit_solution(7276791269935095463)
XLA Ops:
  0.6 0.6 pad_add_fusion.where_ref
  1.2 1.2 %pad_maximum_fusion.scales_ref = f32[2,128]{1,0:T(2,128)} fusion(f32[1,128]{1,0:T(1,128)} %bitcast.9, f32[1,128]{1,0:T(1,128)} %bitcast.10), kind=kLoop, calls=%fused_computation.23 | loop fusion | flops 256 | bytes 2048 | tf_op jit(solution)/shard_map/stack | solution.py:290
  2.4 5.8 %update.1 = (f32[8,2,128,128]{3,2,1,0:T(8,128)}, bf16[4,8,2,32,128]{4,3,2,1,0:T(8,128)(2,1)}) custom-call(s32[2]{0:T(128)} %pad_add_fusion.where_ref, f32[2,128]{1,0:T(2,128)} %pad_maximum_fusion.scales_ref, f32[8,2,128,128]{3,2,1,0:T(8,128)} %state_ref.1, f32[8,2,128,128]{3,2,1,0:T(8,128)} %noise_ref.1), custom_call_target="tpu_custom_call" | custom-call | tf_op jit(solution)/shard_map/update/pallas_call | solution.py:80
  8.2 0.0 copy-start.2
  8.2 6.8 %all-to-all-start = ((bf16[4,8,2,32,128]{4,3,2,1,0:T(8,128)(2,1)}), bf16[4,8,2,32,128]{4,3,2,1,0:T(8,128)(2,1)S(1)}, u32[]{:S(2)}, u32[]{:S(2)}) async-start(bf16[4,8,2,32,128]{4,3,2,1,0:T(8,128)(2,1)} %get-tuple-element.5), calls=%async_computation | async-start | bytes 1048576 | tf_op jit(solution)/shard_map/all_to_all | solution.py:285
  15.0 7.0 %legendre.1.table_ref = bf16[8,512,768]{2,1,0:T(8,128)(2,1)} custom-call(s32[2]{0:T(128)} %pad_add_fusion.where_ref, s32[512]{0:T(512)} %orders_ref.3, f32[2,768]{1,0:T(2,128)} %constant.67.clone.lats_ref, f32[1,512]{1,0:T(1,128)} %constant.68.clone.head_ref), custom_call_target="tpu_custom_call" | custom-call | tf_op jit(solution)/shard_map/legendre/pallas_call | solution.py:158
  22.0 0.9 all-to-all-done.spectra_ref
  22.8 0.0 copy-start.1
  22.8 0.8 copy-done.1
  23.6 5.6 %project.1 = bf16[64,4,24,128]{3,2,1,0:T(8,128)(2,1)} custom-call(s32[2]{0:T(128)} %pad_add_fusion.where_ref, s32[512]{0:T(512)} %orders_ref.3, bf16[4,8,2,32,128]{4,3,2,1,0:T(8,128)(2,1)} %copy-done.1, bf16[8,512,768]{2,1,0:T(8,128)(2,1)} %legendre.1.table_ref), custom_call_target="tpu_custom_call" | custom-call | tf_op jit(solution)/shard_map/project/pallas_call | solution.py:206
  29.2 12.6 %all-to-all-start.1 = ((bf16[64,4,24,128]{3,2,1,0:T(8,128)(2,1)}), bf16[64,4,24,128]{3,2,1,0:T(8,128)(2,1)S(1)}, u32[]{:S(2)}, u32[]{:S(2)}) async-start(bf16[64,4,24,128]{3,2,1,0:T(8,128)(2,1)} %project.1), calls=%async_computation.1 | async-start | bytes 3145728 | tf_op jit(solution)/shard_map/all_to_all | solution.py:297
  41.8 0.0 copy-done.2
  41.8 0.2 reshape.80
  42.0 0.1 copy.9
  42.1 0.1 broadcast_in_dim.15
  42.3 51.7 %fusion.4.fourier_ref = bf16[1024,3072]{1,0:T(8,128)(2,1)} fusion(s32[1024]{0:T(1024)S(1)} %fusion.9, s32[1024]{0:T(1024)S(1)} %bitcast.8, f32[1024]{0:T(1024)S(1)} %select_multiply_fusion), kind=kLoop, calls=%fused_computation.5 | loop fusion | flops 37748736 | bytes 6303744 | tf_op jit(solution)/shard_map/convert_element_type | solution.py:234
  93.9 0.0 all-to-all-done.1.grid_ref
  93.9 0.0 copy-start
  93.9 1.1 %copy-done = bf16[64,4,24,128]{3,2,1,0:T(8,128)(2,1)} copy-done((bf16[64,4,24,128]{3,2,1,0:T(8,128)(2,1)}, bf16[64,4,24,128]{3,2,1,0:T(8,128)(2,1)S(1)}, u32[]{:S(2)}) %copy-start) | copy-done | bytes 1572888
  95.1 13.5 %synthesis.1 = f32[32,24,3072]{2,1,0:T(8,128)} custom-call(s32[2]{0:T(128)} %pad_add_fusion.where_ref, bf16[64,4,24,128]{3,2,1,0:T(8,128)(2,1)} %copy-done, bf16[1024,3072]{1,0:T(8,128)(2,1)} %fusion.4.fourier_ref), custom_call_target="tpu_custom_call" | custom-call | tf_op jit(solution)/shard_map/synthesis/pallas_call | solution.py:264
  (3 shorter events, 0.0 us)
Async XLA Ops:
  8.2 33.6 %copy-start.2 = (s32[512]{0:T(512)S(1)}, s32[512]{0:T(512)}, u32[]{:S(2)}) copy-start(s32[512]{0:T(512)} %orders_ref.3) | copy-start | bytes 6148
  8.2 14.6 %all-to-all-start = ((bf16[4,8,2,32,128]{4,3,2,1,0:T(8,128)(2,1)}), bf16[4,8,2,32,128]{4,3,2,1,0:T(8,128)(2,1)S(1)}, u32[]{:S(2)}, u32[]{:S(2)}) async-start(bf16[4,8,2,32,128]{4,3,2,1,0:T(8,128)(2,1)} %get-tuple-element.5), calls=%async_computation | async-start | bytes 1048576 | tf_op jit(solution)/shard_map/all_to_all | solution.py:285
  22.8 0.8 copy-start.1
  29.2 64.7 %all-to-all-start.1 = ((bf16[64,4,24,128]{3,2,1,0:T(8,128)(2,1)}), bf16[64,4,24,128]{3,2,1,0:T(8,128)(2,1)S(1)}, u32[]{:S(2)}, u32[]{:S(2)}) async-start(bf16[64,4,24,128]{3,2,1,0:T(8,128)(2,1)} %project.1), calls=%async_computation.1 | async-start | bytes 3145728 | tf_op jit(solution)/shard_map/all_to_all | solution.py:297
  93.9 1.1 %copy-start = (bf16[64,4,24,128]{3,2,1,0:T(8,128)(2,1)}, bf16[64,4,24,128]{3,2,1,0:T(8,128)(2,1)S(1)}, u32[]{:S(2)}) copy-start(bf16[64,4,24,128]{3,2,1,0:T(8,128)(2,1)S(1)} %all-to-all-done.1.grid_ref) | copy-start | bytes 4718596
where the time goes:
time: 109 us
  other arithmetic  53.5 us (49%)
  Pallas kernels  31.9 us (29%)
  starting transfers between devices  19.3 us (18%)
  local copies, waits for them, and re-layouts  2.34 us (2%)
    convert_element_type x1, other arithmetic, fourier_table(): return (weight * jnp.cos(angles)).astype(jnp.bfloat16)  51.7 us
    pallas_call x1, Pallas kernels, synthesize(): pl.pallas_call(synthesis_kernel, grid=(NLON // WIDTH,), in_specs=[pl.Bloc...  13.5 us
    all_to_all x1, starting transfers between devices, on_device(): grid_spec = lax.all_to_all(grid_spec, 'lat', 0, 0, tiled=True)  12.6 us
    pallas_call x1, Pallas kernels, legendre_table(): pl.pallas_call(table_kernel, grid=(M // CHUNK,), in_specs=[pl.BlockSpec(m...  6.96 us
    all_to_all x1, starting transfers between devices, exchanged(): return lax.all_to_all(spectra, 'scale', 0, 0, tiled=True)  6.77 us
    pallas_call x1, Pallas kernels, update(): pl.pallas_call(update_kernel, grid=(SLOTS,), in_specs=[pl.BlockSpec(memor...  5.8 us
    pallas_call x1, Pallas kernels, project(): pl.pallas_call(project_kernel, grid=(PAIRS,), in_specs=[pl.BlockSpec(memo...  5.58 us
  transfers between devices with their start and end apart: 2, of which 1 were waited for; matrix products, arithmetic and copies ran while one was open for 48% of the time, Pallas kernels for 6%

commit v1 on v0

--- a/solution.py
+++ b/solution.py
@@ -21,6 +21,7 @@
 OWN_FIELDS = FIELDS // SCALE_PARTS
 PAIRS = SLOTS // 2
 CHUNK = 128
+GROUP = 2
 WIDTH = 512
 
 log_floor = -60.0
@@ -50,15 +51,13 @@
     return head.astype(np.float32)[None]
 
 
-def update_kernel(where_ref, scales_ref, state_ref, noise_ref, new_ref, spectra_ref, factor):
+def update_kernel(time_ref, length_ref, state_ref, noise_ref, new_ref, spectra_ref, factor):
     @pl.when(pl.program_id(0) == 0)
     def _():
-        time_row = jnp.broadcast_to(scales_ref[0:1, :], (FIELDS, FIELDS))
-        length_row = jnp.broadcast_to(scales_ref[1:2, :], (FIELDS, FIELDS))
-        timescale = time_row.T
-        lengthscale = length_row.T
+        timescale = jnp.broadcast_to(time_ref[...], (FIELDS, FIELDS)).T
+        lengthscale = jnp.broadcast_to(length_ref[...], (FIELDS, FIELDS)).T
         decay = jnp.exp(-1.0 / timescale)
-        first = where_ref[1] * CHUNK
+        first = lax.axis_index("scale") * CHUNK
         degree = (first + lax.broadcasted_iota(jnp.int32, (FIELDS, CHUNK), 1)).astype(jnp.float32)
         factor[0] = decay
         factor[1] = (
@@ -67,28 +66,27 @@
             * (M / lengthscale)
         )
 
-    for part in range(2):
-        new = factor[0] * state_ref[0, part] + factor[1] * noise_ref[0, part]
-        new_ref[0, part] = new
-        rounded = new.astype(jnp.bfloat16)
-        for owner in range(SCALE_PARTS):
-            spectra_ref[owner, 0, part] = rounded[owner * OWN_FIELDS : (owner + 1) * OWN_FIELDS]
-
-
-def update(where, scales, state, noise):
-    block = pl.BlockSpec((1, 2, FIELDS, CHUNK), lambda s: (s, 0, 0, 0))
+    for slot in range(GROUP):
+        for part in range(2):
+            new = factor[0] * state_ref[slot, part] + factor[1] * noise_ref[slot, part]
+            new_ref[slot, part] = new
+            rounded = new.astype(jnp.bfloat16)
+            for owner in range(SCALE_PARTS):
+                spectra_ref[owner, slot, part] = rounded[
+                    owner * OWN_FIELDS : (owner + 1) * OWN_FIELDS
+                ]
+
+
+def update(timescale, lengthscale, state, noise):
+    block = pl.BlockSpec((GROUP, 2, FIELDS, CHUNK), lambda s: (s, 0, 0, 0))
+    line = pl.BlockSpec((1, FIELDS), lambda s: (0, 0))
     return pl.pallas_call(
         update_kernel,
-        grid=(SLOTS,),
-        in_specs=[
-            pl.BlockSpec(memory_space=pltpu.SMEM),
-            pl.BlockSpec((2, FIELDS), lambda s: (0, 0)),
-            block,
-            block,
-        ],
+        grid=(SLOTS // GROUP,),
+        in_specs=[line, line, block, block],
         out_specs=[
             block,
-            pl.BlockSpec((SCALE_PARTS, 1, 2, OWN_FIELDS, CHUNK), lambda s: (0, s, 0, 0, 0)),
+            pl.BlockSpec((SCALE_PARTS, GROUP, 2, OWN_FIELDS, CHUNK), lambda s: (0, s, 0, 0, 0)),
         ],
         out_shape=[
             jax.ShapeDtypeStruct((SLOTS, 2, FIELDS, CHUNK), jnp.float32),
@@ -97,14 +95,14 @@
         scratch_shapes=[pltpu.VMEM((2, FIELDS, CHUNK), jnp.float32)],
         compiler_params=vmem_params("arbitrary"),
         name="update",
-    )(where, scales, state, noise)
-
-
-def own_orders(where_ref, orders_ref, shape):
+    )(timescale, lengthscale, state, noise)
+
+
+def own_orders(orders_ref, shape):
     slot = lax.broadcasted_iota(jnp.int32, shape, 0)
     orders = jnp.zeros(shape, jnp.int32)
     for s in range(SLOTS):
-        orders = jnp.where(slot == s, orders_ref[where_ref[0] * SLOTS + s], orders)
+        orders = jnp.where(slot == s, orders_ref[lax.axis_index("lat") * SLOTS + s], orders)
     return orders
 
 
@@ -113,14 +111,14 @@
     return jnp.sqrt(jnp.maximum(squared - orders * orders, 0.0) / (4.0 * squared - 1.0))
 
 
-def table_kernel(where_ref, orders_ref, lats_ref, head_ref, table_ref, rows, carried, pole):
+def table_kernel(orders_ref, lats_ref, head_ref, table_ref, rows, carried, pole):
     step = pl.program_id(0)
-    order_tile = own_orders(where_ref, orders_ref, (SLOTS, LANES))
+    order_tile = own_orders(orders_ref, (SLOTS, LANES))
     order_real = order_tile.astype(jnp.float32)
 
     @pl.when(step == 0)
     def _():
-        wide = own_orders(where_ref, orders_ref, (SLOTS, M))
+        wide = own_orders(orders_ref, (SLOTS, M))
         chosen = lax.broadcasted_iota(jnp.int32, (SLOTS, M), 1) == wide
         head = jnp.sum(jnp.where(chosen, head_ref[...], 0.0), axis=1, keepdims=True)
         log_start = head + order_real[:, :1] * lats_ref[1:2, :]
@@ -154,12 +152,11 @@
             ].astype(jnp.bfloat16)
 
 
-def legendre_table(where, orders, lats, head):
+def legendre_table(orders, lats, head):
     return pl.pallas_call(
         table_kernel,
         grid=(M // CHUNK,),
         in_specs=[
-            pl.BlockSpec(memory_space=pltpu.SMEM),
             pl.BlockSpec(memory_space=pltpu.SMEM),
             pl.BlockSpec((2, HALF), lambda i: (0, 0)),
             pl.BlockSpec((1, M), lambda i: (0, 0)),
@@ -173,19 +170,19 @@
         ],
         compiler_params=vmem_params("arbitrary"),
         name="legendre",
-    )(where, orders, lats, head)
-
-
-def project_kernel(where_ref, orders_ref, spectra_ref, table_ref, out_ref):
+    )(orders, lats, head)
+
+
+def project_kernel(orders_ref, spectra_ref, table_ref, out_ref):
     pair = pl.program_id(0)
     north = []
     south = []
     lane = lax.broadcasted_iota(jnp.int32, (1, CHUNK), 1)
     for half in range(2):
-        order = orders_ref[where_ref[0] * SLOTS + 2 * pair + half]
+        order = orders_ref[lax.axis_index("lat") * SLOTS + 2 * pair + half]
         sign = (1 - 2 * ((lane + order) % 2)).astype(jnp.float32).astype(jnp.bfloat16)
         blocks = [
-            spectra_ref[b, half].reshape(2 * OWN_FIELDS, CHUNK) for b in range(SCALE_PARTS)
+            spectra_ref[b, 2 * pair + half].reshape(2 * OWN_FIELDS, CHUNK) for b in range(SCALE_PARTS)
         ]
         left = jnp.concatenate(
             [jnp.concatenate([b, b * sign], axis=0) for b in blocks], axis=1
@@ -202,43 +199,63 @@
         out_ref[LAT_PARTS - 1 - d, 0] = lower[d]
 
 
-def project(where, orders, spectra, table):
+def project(orders, spectra, table):
     return pl.pallas_call(
         project_kernel,
         grid=(PAIRS,),
         in_specs=[
             pl.BlockSpec(memory_space=pltpu.SMEM),
-            pl.BlockSpec(memory_space=pltpu.SMEM),
-            pl.BlockSpec(
-                (SCALE_PARTS, 2, 2, OWN_FIELDS, CHUNK), lambda p: (0, p, 0, 0, 0)
-            ),
+            pl.BlockSpec(memory_space=pltpu.VMEM),
             pl.BlockSpec((2, M, HALF), lambda p: (p, 0, 0)),
         ],
         out_specs=pl.BlockSpec((LAT_PARTS, 1, ROWS, LANES), lambda p: (0, p, 0, 0)),
         out_shape=jax.ShapeDtypeStruct((LAT_PARTS, PAIRS, ROWS, LANES), jnp.bfloat16),
         compiler_params=vmem_params("arbitrary"),
         name="project",
-    )(where, orders, spectra, table)
+    )(orders, spectra, table)
+
+
+def remainder(value, divisor):
+    return value - divisor * jnp.floor(value * (1.0 / divisor))
+
+
+def fourier_kernel(orders_ref, table_ref):
+    order = jnp.broadcast_to(orders_ref[0], (LANES, LANES)).T
+    lane = lax.broadcasted_iota(jnp.int32, (LANES, LANES), 1).astype(jnp.float32)
+    weight = jnp.where(order == 0.0, 1.0, 2.0) / M
+    fine = remainder(order * lane, float(NLON)) * (2.0 * math.pi / NLON)
+    coarse = remainder(order * lane, float(NLON // LANES)) * (2.0 * math.pi * LANES / NLON)
+    fine_cos = jnp.cos(fine)
+    fine_sin = jnp.sin(fine)
+    coarse_cos = weight * jnp.cos(coarse)
+    coarse_sin = weight * jnp.sin(coarse)
+    for a in range(NLON // LANES):
+        cos_a = coarse_cos[:, a : a + 1]
+        sin_a = coarse_sin[:, a : a + 1]
+        lanes = slice(a * LANES, (a + 1) * LANES)
+        table_ref[:LANES, lanes] = (cos_a * fine_cos - sin_a * fine_sin).astype(jnp.bfloat16)
+        table_ref[LANES:, lanes] = (-sin_a * fine_cos - cos_a * fine_sin).astype(jnp.bfloat16)
 
 
 def fourier_table(slot_wavenumber):
     orders = slot_wavenumber.reshape(LAT_PARTS, 2, 2, 2).transpose(1, 3, 2, 0)
-    orders = orders.reshape(2, 2, 1, 2 * LAT_PARTS)
-    orders = jnp.broadcast_to(orders, (2, 2, 2, 2 * LAT_PARTS)).reshape(2 * M, 1)
-    row = lax.broadcasted_iota(jnp.int32, (2 * M, 1), 0)
-    quarter = (row // (2 * LAT_PARTS)) % 2 * (NLON // 4)
-    points = lax.broadcasted_iota(jnp.int32, (1, NLON), 1)
-    phase_index = (orders * points + quarter) % NLON
-    angles = phase_index.astype(jnp.float32) * (2.0 * math.pi / NLON)
-    weight = jnp.where(orders == 0, 1.0, 2.0) / M
-    return (weight * jnp.cos(angles)).astype(jnp.bfloat16)
-
-
-def synthesis_kernel(where_ref, grid_ref, fourier_ref, out_ref, wide, turned, left):
+    orders = orders.reshape(4, 1, 2 * LAT_PARTS).astype(jnp.float32)
+    return pl.pallas_call(
+        fourier_kernel,
+        grid=(4,),
+        in_specs=[pl.BlockSpec((1, 1, LANES), lambda i: (i, 0, 0))],
+        out_specs=pl.BlockSpec((2 * LANES, NLON), lambda i: (i, 0)),
+        out_shape=jax.ShapeDtypeStruct((2 * M, NLON), jnp.bfloat16),
+        compiler_params=vmem_params("arbitrary"),
+        name="fourier",
+    )(orders)
+
+
+def synthesis_kernel(grid_ref, fourier_ref, out_ref, wide, turned, left):
     @pl.when(pl.program_id(0) == 0)
     def _():
         wide[...] = grid_ref[...].astype(jnp.float32).reshape(wide.shape)
-        is_south = where_ref[0] >= LAT_PARTS // 2
+        is_south = lax.axis_index("lat") >= LAT_PARTS // 2
         for row in range(ROWS):
             target = jnp.where(is_south, ROWS - 1 - row, row)
             for group in range(2):
@@ -260,13 +277,12 @@
     out_ref[...] = product.reshape(out_ref.shape)
 
 
-def synthesize(where, grid_spec, fourier):
+def synthesize(grid_spec, fourier):
     return pl.pallas_call(
         synthesis_kernel,
         grid=(NLON // WIDTH,),
         in_specs=[
-            pl.BlockSpec(memory_space=pltpu.SMEM),
-            pl.BlockSpec((LAT_PARTS, PAIRS, ROWS, LANES), lambda k: (0, 0, 0, 0)),
+            pl.BlockSpec(memory_space=pltpu.VMEM),
             pl.BlockSpec((2 * M, WIDTH), lambda k: (0, k)),
         ],
         out_specs=pl.BlockSpec((OWN_FIELDS, ROWS, WIDTH), lambda k: (0, 0, k)),
@@ -278,7 +294,7 @@
         ],
         compiler_params=vmem_params("arbitrary"),
         name="synthesis",
-    )(where, grid_spec, fourier)
+    )(grid_spec, fourier)
 
 
 def exchanged(spectra):
@@ -286,16 +302,14 @@
 
 
 def on_device(state, noise, slot_wavenumber, timescale, lengthscale):
-    where = jnp.stack([lax.axis_index("lat"), lax.axis_index("scale")])
-    scales = jnp.stack([timescale, lengthscale])
     lats = jnp.asarray(latitude_constants())
     head = jnp.asarray(log_head_table())
-    new_state, spectra = update(where, scales, state, noise)
+    new_state, spectra = update(timescale[None], lengthscale[None], state, noise)
     spectra = exchanged(spectra)
-    table = legendre_table(where, slot_wavenumber, lats, head)
-    grid_spec = project(where, slot_wavenumber, spectra, table)
+    table = legendre_table(slot_wavenumber, lats, head)
+    grid_spec = project(slot_wavenumber, spectra, table)
     grid_spec = lax.all_to_all(grid_spec, "lat", 0, 0, tiled=True)
-    pattern = synthesize(where, grid_spec, fourier_table(slot_wavenumber))
+    pattern = synthesize(grid_spec, fourier_table(slot_wavenumber))
     return (new_state, pattern)
 
 

time: 109 us -> 94.1 us (0.86)
  other arithmetic: 53.5 us -> 0.01 us
  waiting for transfers between devices: 0.89 us -> 31.9 us
  Pallas kernels: 31.9 us -> 38.8 us
    convert_element_type x1, other arithmetic: 51.7 us -> 0.01 us  [fourier_table(): orders = orders.reshape(4, 1, 2 * LAT_PARTS).astype(jnp.float32)]
    all_to_all x1, waiting for transfers between devices: 0.01 us -> 31.1 us  [on_device(): grid_spec = lax.all_to_all(grid_spec, 'lat', 0, 0, tiled=True)]
    pallas_call x1 -> x2, Pallas kernels: 5.8 us -> 12.8 us  [the longest x1 9 us: fourier_table(): pl.pallas_call(fourier_kernel, grid=(4,), in_specs=[pl.BlockSpec((1, 1, L...]
    another operation x2 -> x0, other arithmetic: 1.8 us -> none  [the longest x1 1.24 us: on_device(): scales = jnp.stack([timescale, lengthscale])]
  transfers between devices with their start and end apart: 2 -> 2, of which waited for: 1 -> 2; matrix products, arithmetic and copies ran while one was open for 48% -> 1% of each run, Pallas kernels for 6% -> 17%
where the time goes in v1:
time: 94.1 us; the launch traced here: 93.6 us
  Pallas kernels  38.8 us (41%)
  waiting for transfers between devices  31.9 us (34%)
  starting transfers between devices  19.2 us (20%)
  local copies, waits for them, and re-layouts  2.93 us (3%)
    all_to_all x1, waiting for transfers between devices, on_device(): grid_spec = lax.all_to_all(grid_spec, 'lat', 0, 0, tiled=True)  31.1 us
    pallas_call x1, Pallas kernels, synthesize(): pl.pallas_call(synthesis_kernel, grid=(NLON // WIDTH,), in_specs=[pl.Bloc...  13.5 us
    all_to_all x1, starting transfers between devices, on_device(): grid_spec = lax.all_to_all(grid_spec, 'lat', 0, 0, tiled=True)  12.6 us
    pallas_call x1, Pallas kernels, fourier_table(): pl.pallas_call(fourier_kernel, grid=(4,), in_specs=[pl.BlockSpec((1, 1, L...  9 us
    pallas_call x1, Pallas kernels, legendre_table(): pl.pallas_call(table_kernel, grid=(M // CHUNK,), in_specs=[pl.BlockSpec(m...  6.98 us
    all_to_all x1, starting transfers between devices, exchanged(): return lax.all_to_all(spectra, 'scale', 0, 0, tiled=True)  6.64 us
    pallas_call x1, Pallas kernels, project(): pl.pallas_call(project_kernel, grid=(PAIRS,), in_specs=[pl.BlockSpec(memo...  5.53 us
    pallas_call x1, Pallas kernels, update(): pl.pallas_call(update_kernel, grid=(SLOTS // GROUP,), in_specs=[line, lin...  3.81 us
  transfers between devices with their start and end apart: 2, of which 2 were waited for; matrix products, arithmetic and copies ran while one was open for 1% of the time, Pallas kernels for 17%

profile of v1, /device:TPU:1, one launch (start us, length us, event | category | flops | bytes accessed | tf_op | source)
XLA Modules:
  0.0 93.6 jit_solution(2052877177476659935)
XLA Ops:
  0.6 3.8 %update.1 = (f32[8,2,128,128]{3,2,1,0:T(8,128)}, bf16[4,8,2,32,128]{4,3,2,1,0:T(8,128)(2,1)}) custom-call(f32[1,128]{1,0:T(1,128)} %bitcast.4, f32[1,128]{1,0:T(1,128)} %bitcast.5, f32[8,2,128,128]{3,2,1,0:T(8,128)} %state_ref.1, f32[8,2,128,128]{3,2,1,0:T(8,128)} %noise_ref.1), custom_call_target="tpu_custom_call" | custom-call | tf_op jit(solution)/shard_map/update/pallas_call | solution.py:83
  4.4 6.6 %all-to-all-start = ((bf16[4,8,2,32,128]{4,3,2,1,0:T(8,128)(2,1)}), bf16[4,8,2,32,128]{4,3,2,1,0:T(8,128)(2,1)S(1)}, u32[]{:S(2)}, u32[]{:S(2)}) async-start(bf16[4,8,2,32,128]{4,3,2,1,0:T(8,128)(2,1)} %get-tuple-element.5), calls=%async_computation | async-start | bytes 1048576 | tf_op jit(solution)/shard_map/all_to_all | solution.py:301
  11.1 7.0 %legendre.1.table_ref = bf16[8,512,768]{2,1,0:T(8,128)(2,1)} custom-call(s32[512]{0:T(512)} %orders_ref.3, f32[2,768]{1,0:T(2,128)} %constant.4.clone.lats_ref, f32[1,512]{1,0:T(1,128)} %constant.5.clone.head_ref), custom_call_target="tpu_custom_call" | custom-call | tf_op jit(solution)/shard_map/legendre/pallas_call | solution.py:156
  18.1 0.0 copy-start.2
  18.1 0.9 all-to-all-done.spectra_ref
  18.9 0.0 copy-start.1
  18.9 0.8 copy-done.1
  19.7 5.5 %project.1 = bf16[64,4,24,128]{3,2,1,0:T(8,128)(2,1)} custom-call(s32[512]{0:T(512)} %orders_ref.3, bf16[4,8,2,32,128]{4,3,2,1,0:T(8,128)(2,1)} %copy-done.1, bf16[8,512,768]{2,1,0:T(8,128)(2,1)} %legendre.1.table_ref), custom_call_target="tpu_custom_call" | custom-call | tf_op jit(solution)/shard_map/project/pallas_call | solution.py:203
  25.3 12.6 %all-to-all-start.1 = ((bf16[64,4,24,128]{3,2,1,0:T(8,128)(2,1)}), bf16[64,4,24,128]{3,2,1,0:T(8,128)(2,1)S(1)}, u32[]{:S(2)}, u32[]{:S(2)}) async-start(bf16[64,4,24,128]{3,2,1,0:T(8,128)(2,1)} %project.1), calls=%async_computation.1 | async-start | bytes 3145728 | tf_op jit(solution)/shard_map/all_to_all | solution.py:311
  37.8 0.0 copy-done.2
  37.9 0.2 convert_element_type.10
  38.1 0.1 copy.9
  38.2 0.7 convert_element_type.12.orders_ref
  38.9 9.0 %fourier.1.fourier_ref = bf16[1024,3072]{1,0:T(8,128)(2,1)} custom-call(f32[4,1,128]{2,1,0:T(1,128)} %convert_element_type.12.orders_ref), custom_call_target="tpu_custom_call" | custom-call | tf_op jit(solution)/shard_map/fourier/pallas_call | solution.py:243
  47.9 31.1 %all-to-all-done.1.grid_ref = bf16[64,4,24,128]{3,2,1,0:T(8,128)(2,1)S(1)} async-done(((bf16[64,4,24,128]{3,2,1,0:T(8,128)(2,1)}), bf16[64,4,24,128]{3,2,1,0:T(8,128)(2,1)S(1)}, u32[]{:S(2)}, u32[]{:S(2)}) %all-to-all-start.1) | async-done | bytes 1572896 | tf_op jit(solution)/shard_map/all_to_all | solution.py:311
  78.9 0.0 copy-start
  78.9 1.1 %copy-done = bf16[64,4,24,128]{3,2,1,0:T(8,128)(2,1)} copy-done((bf16[64,4,24,128]{3,2,1,0:T(8,128)(2,1)}, bf16[64,4,24,128]{3,2,1,0:T(8,128)(2,1)S(1)}, u32[]{:S(2)}) %copy-start) | copy-done | bytes 1572888
  80.1 13.5 %synthesis.1 = f32[32,24,3072]{2,1,0:T(8,128)} custom-call(bf16[64,4,24,128]{3,2,1,0:T(8,128)(2,1)} %copy-done, bf16[1024,3072]{1,0:T(8,128)(2,1)} %fourier.1.fourier_ref), custom_call_target="tpu_custom_call" | custom-call | tf_op jit(solution)/shard_map/synthesis/pallas_call | solution.py:281
  (1 shorter events, 0.0 us)
Async XLA Ops:
  4.4 14.5 %all-to-all-start = ((bf16[4,8,2,32,128]{4,3,2,1,0:T(8,128)(2,1)}), bf16[4,8,2,32,128]{4,3,2,1,0:T(8,128)(2,1)S(1)}, u32[]{:S(2)}, u32[]{:S(2)}) async-start(bf16[4,8,2,32,128]{4,3,2,1,0:T(8,128)(2,1)} %get-tuple-element.5), calls=%async_computation | async-start | bytes 1048576 | tf_op jit(solution)/shard_map/all_to_all | solution.py:301
  18.1 19.8 %copy-start.2 = (s32[512]{0:T(512)S(1)}, s32[512]{0:T(512)}, u32[]{:S(2)}) copy-start(s32[512]{0:T(512)} %orders_ref.3) | copy-start | bytes 6148
  18.9 0.8 copy-start.1
  25.3 53.7 %all-to-all-start.1 = ((bf16[64,4,24,128]{3,2,1,0:T(8,128)(2,1)}), bf16[64,4,24,128]{3,2,1,0:T(8,128)(2,1)S(1)}, u32[]{:S(2)}, u32[]{:S(2)}) async-start(bf16[64,4,24,128]{3,2,1,0:T(8,128)(2,1)} %project.1), calls=%async_computation.1 | async-start | bytes 3145728 | tf_op jit(solution)/shard_map/all_to_all | solution.py:311
  78.9 1.1 %copy-start = (bf16[64,4,24,128]{3,2,1,0:T(8,128)(2,1)}, bf16[64,4,24,128]{3,2,1,0:T(8,128)(2,1)S(1)}, u32[]{:S(2)}) copy-start(bf16[64,4,24,128]{3,2,1,0:T(8,128)(2,1)S(1)} %all-to-all-done.1.grid_ref) | copy-start | bytes 4718596

commit v2 on v1

--- a/solution.py
+++ b/solution.py
@@ -1,3 +1,4 @@
+import functools
 import math
 
 import jax
@@ -23,14 +24,18 @@
 CHUNK = 128
 GROUP = 2
 WIDTH = 512
+PITCH = PAIRS * ROWS + 8
+BANDS = ((0, 8), (8, 16))
 
 log_floor = -60.0
 
 
-def vmem_params(*semantics):
-    return pltpu.CompilerParams(
-        dimension_semantics=semantics, vmem_limit_bytes=56 * 1024 * 1024
-    )
+whole = pl.BlockSpec(memory_space=pltpu.VMEM)
+outside = pl.BlockSpec(memory_space=pltpu.HBM)
+
+
+def vmem_params(mebibytes, **others):
+    return pltpu.CompilerParams(vmem_limit_bytes=mebibytes * 1024 * 1024, **others)
 
 
 def latitude_constants():
@@ -93,7 +98,7 @@
             jax.ShapeDtypeStruct((SCALE_PARTS, SLOTS, 2, OWN_FIELDS, CHUNK), jnp.bfloat16),
         ],
         scratch_shapes=[pltpu.VMEM((2, FIELDS, CHUNK), jnp.float32)],
-        compiler_params=vmem_params("arbitrary"),
+        compiler_params=vmem_params(58, dimension_semantics=("arbitrary",)),
         name="update",
     )(timescale, lengthscale, state, noise)
 
@@ -168,49 +173,55 @@
             pltpu.VMEM((2, SLOTS, HALF), jnp.float32),
             pltpu.VMEM((SLOTS, HALF), jnp.float32),
         ],
-        compiler_params=vmem_params("arbitrary"),
+        compiler_params=vmem_params(58, dimension_semantics=("arbitrary",)),
         name="legendre",
     )(orders, lats, head)
 
 
-def project_kernel(orders_ref, spectra_ref, table_ref, out_ref):
-    pair = pl.program_id(0)
-    north = []
-    south = []
+def project_kernel(orders_ref, spectra_ref, table_ref, out_ref, table, arrived):
     lane = lax.broadcasted_iota(jnp.int32, (1, CHUNK), 1)
-    for half in range(2):
-        order = orders_ref[lax.axis_index("lat") * SLOTS + 2 * pair + half]
-        sign = (1 - 2 * ((lane + order) % 2)).astype(jnp.float32).astype(jnp.bfloat16)
-        blocks = [
-            spectra_ref[b, 2 * pair + half].reshape(2 * OWN_FIELDS, CHUNK) for b in range(SCALE_PARTS)
-        ]
-        left = jnp.concatenate(
-            [jnp.concatenate([b, b * sign], axis=0) for b in blocks], axis=1
-        )
-        product = jnp.dot(left, table_ref[half], preferred_element_type=jnp.float32)
-        north.append(product[: 2 * OWN_FIELDS])
-        south.append(product[2 * OWN_FIELDS :])
-    upper = jnp.concatenate(north, axis=0).T.reshape(LAT_PARTS // 2, ROWS, LANES)
-    lower = jnp.concatenate(south, axis=0).T.reshape(LAT_PARTS // 2, ROWS, LANES)
-    upper = upper.astype(jnp.bfloat16)
-    lower = lower.astype(jnp.bfloat16)
-    for d in range(LAT_PARTS // 2):
-        out_ref[d, 0] = upper[d]
-        out_ref[LAT_PARTS - 1 - d, 0] = lower[d]
+    copies = [
+        pltpu.make_async_copy(table_ref.at[s], table.at[s], arrived.at[s]) for s in range(SLOTS)
+    ]
+    for copy in copies:
+        copy.start()
+    for pair in range(PAIRS):
+        north = []
+        south = []
+        for half in range(2):
+            order = orders_ref[lax.axis_index("lat") * SLOTS + 2 * pair + half]
+            sign = (1 - 2 * ((lane + order) % 2)).astype(jnp.float32).astype(jnp.bfloat16)
+            blocks = [
+                spectra_ref[b, 2 * pair + half].reshape(2 * OWN_FIELDS, CHUNK)
+                for b in range(SCALE_PARTS)
+            ]
+            left = jnp.concatenate(
+                [jnp.concatenate([b, b * sign], axis=0) for b in blocks], axis=1
+            )
+            copies[2 * pair + half].wait()
+            product = jnp.dot(left, table[2 * pair + half], preferred_element_type=jnp.float32)
+            north.append(product[: 2 * OWN_FIELDS])
+            south.append(product[2 * OWN_FIELDS :])
+        upper = jnp.concatenate(north, axis=0).T.reshape(LAT_PARTS // 2, ROWS, LANES)
+        lower = jnp.concatenate(south, axis=0).T.reshape(LAT_PARTS // 2, ROWS, LANES)
+        upper = upper.astype(jnp.bfloat16)
+        lower = lower.astype(jnp.bfloat16)
+        for d in range(LAT_PARTS // 2):
+            out_ref[d, pair] = upper[d]
+            out_ref[LAT_PARTS - 1 - d, pair] = lower[d]
 
 
 def project(orders, spectra, table):
     return pl.pallas_call(
         project_kernel,
-        grid=(PAIRS,),
-        in_specs=[
-            pl.BlockSpec(memory_space=pltpu.SMEM),
-            pl.BlockSpec(memory_space=pltpu.VMEM),
-            pl.BlockSpec((2, M, HALF), lambda p: (p, 0, 0)),
-        ],
-        out_specs=pl.BlockSpec((LAT_PARTS, 1, ROWS, LANES), lambda p: (0, p, 0, 0)),
+        in_specs=[pl.BlockSpec(memory_space=pltpu.SMEM), whole, outside],
+        out_specs=whole,
         out_shape=jax.ShapeDtypeStruct((LAT_PARTS, PAIRS, ROWS, LANES), jnp.bfloat16),
-        compiler_params=vmem_params("arbitrary"),
+        scratch_shapes=[
+            pltpu.VMEM((SLOTS, M, HALF), jnp.bfloat16),
+            pltpu.SemaphoreType.DMA((SLOTS,)),
+        ],
+        compiler_params=vmem_params(52),
         name="project",
     )(orders, spectra, table)
 
@@ -246,53 +257,98 @@
         in_specs=[pl.BlockSpec((1, 1, LANES), lambda i: (i, 0, 0))],
         out_specs=pl.BlockSpec((2 * LANES, NLON), lambda i: (i, 0)),
         out_shape=jax.ShapeDtypeStruct((2 * M, NLON), jnp.bfloat16),
-        compiler_params=vmem_params("arbitrary"),
+        compiler_params=vmem_params(58, dimension_semantics=("arbitrary",)),
         name="fourier",
     )(orders)
 
 
-def synthesis_kernel(grid_ref, fourier_ref, out_ref, wide, turned, left):
-    @pl.when(pl.program_id(0) == 0)
-    def _():
-        wide[...] = grid_ref[...].astype(jnp.float32).reshape(wide.shape)
-        is_south = lax.axis_index("lat") >= LAT_PARTS // 2
-        for row in range(ROWS):
-            target = jnp.where(is_south, ROWS - 1 - row, row)
-            for group in range(2):
-                stacked = jnp.concatenate(
-                    [
-                        wide[pl.ds((2 * group + t) * ROWS + row, LAT_PARTS, stride=PAIRS * ROWS), :]
-                        for t in range(2)
-                    ],
-                    axis=0,
-                ).T
-                for q in range(4):
-                    turned[4 * group + q, pl.ds(target, OWN_FIELDS, stride=ROWS), :] = stacked[
-                        q * OWN_FIELDS : (q + 1) * OWN_FIELDS
-                    ]
-        for q in range(8):
-            left[:, q * LANES : (q + 1) * LANES] = turned[q].astype(jnp.bfloat16)
-
-    product = jnp.dot(left[...], fourier_ref[...], preferred_element_type=jnp.float32)
-    out_ref[...] = product.reshape(out_ref.shape)
+def synthesis_kernel(
+    grid_ref, fourier_ref, out_ref, wide, turned, left, done, fourier, arrived, fetched
+):
+    fetches = []
+    for k in range(NLON // WIDTH):
+        points = slice(k * WIDTH, (k + 1) * WIDTH)
+        fetches.append(
+            pltpu.make_async_copy(
+                fourier_ref.at[:, points], fourier.at[:, points], fetched.at[k]
+            )
+        )
+        fetches[k].start()
+    for source in range(LAT_PARTS):
+        wide[source * PITCH : source * PITCH + PAIRS * ROWS, :] = (
+            grid_ref[source].astype(jnp.float32).reshape(PAIRS * ROWS, LANES)
+        )
+    is_south = lax.axis_index("lat") >= LAT_PARTS // 2
+
+    def transpose(first, count, row, group):
+        source_row = jnp.where(is_south, ROWS - 1 - (first + row), first + row)
+        stacked = jnp.concatenate(
+            [
+                wide[pl.ds((2 * group + t) * ROWS + source_row, LAT_PARTS, stride=PITCH), :]
+                for t in range(2)
+            ],
+            axis=0,
+        ).T
+        for q in range(4):
+            turned[
+                4 * group + q, pl.ds(OWN_FIELDS * first + row, OWN_FIELDS, stride=count), :
+            ] = stacked[q * OWN_FIELDS : (q + 1) * OWN_FIELDS]
+
+    def narrow(first, count, q):
+        rows = slice(OWN_FIELDS * first, OWN_FIELDS * (first + count))
+        left[rows, q * LANES : (q + 1) * LANES] = turned[q, rows, :].astype(jnp.bfloat16)
+
+    def preparation(first, count):
+        steps = []
+        for group in range(2):
+            steps += [
+                functools.partial(transpose, first, count, row, group) for row in range(count)
+            ]
+            steps += [functools.partial(narrow, first, count, 4 * group + q) for q in range(4)]
+        return steps
+
+    copies = []
+    for step in preparation(*BANDS[0]):
+        step()
+    for band, (first, count) in enumerate(BANDS):
+        rows = slice(OWN_FIELDS * first, OWN_FIELDS * (first + count))
+        pending = preparation(*BANDS[band + 1]) if band + 1 < len(BANDS) else []
+        share = -(-len(pending) // (NLON // WIDTH))
+        for k in range(NLON // WIDTH):
+            points = slice(k * WIDTH, (k + 1) * WIDTH)
+            if band == 0:
+                fetches[k].wait()
+            product = jnp.dot(left[rows, :], fourier[:, points], preferred_element_type=jnp.float32)
+            done[:, first : first + count, points] = product.reshape(OWN_FIELDS, count, WIDTH)
+            copy = pltpu.make_async_copy(
+                done.at[:, first : first + count, points],
+                out_ref.at[:, first : first + count, points],
+                arrived.at[len(copies)],
+            )
+            copy.start()
+            copies.append(copy)
+            for step in pending[k * share : (k + 1) * share]:
+                step()
+    for copy in copies:
+        copy.wait()
 
 
 def synthesize(grid_spec, fourier):
     return pl.pallas_call(
         synthesis_kernel,
-        grid=(NLON // WIDTH,),
-        in_specs=[
-            pl.BlockSpec(memory_space=pltpu.VMEM),
-            pl.BlockSpec((2 * M, WIDTH), lambda k: (0, k)),
-        ],
-        out_specs=pl.BlockSpec((OWN_FIELDS, ROWS, WIDTH), lambda k: (0, 0, k)),
+        in_specs=[whole, outside],
+        out_specs=outside,
         out_shape=jax.ShapeDtypeStruct((OWN_FIELDS, ROWS, NLON), jnp.float32),
         scratch_shapes=[
-            pltpu.VMEM((LAT_PARTS * PAIRS * ROWS, LANES), jnp.float32),
+            pltpu.VMEM((LAT_PARTS * PITCH, LANES), jnp.float32),
             pltpu.VMEM((8, OWN_FIELDS * ROWS, LANES), jnp.float32),
             pltpu.VMEM((OWN_FIELDS * ROWS, 2 * M), jnp.bfloat16),
-        ],
-        compiler_params=vmem_params("arbitrary"),
+            pltpu.VMEM((OWN_FIELDS, ROWS, NLON), jnp.float32),
+            pltpu.VMEM((2 * M, NLON), jnp.bfloat16),
+            pltpu.SemaphoreType.DMA((len(BANDS) * (NLON // WIDTH),)),
+            pltpu.SemaphoreType.DMA((NLON // WIDTH,)),
+        ],
+        compiler_params=vmem_params(52),
         name="synthesis",
     )(grid_spec, fourier)
 

time: 94.1 us -> 88.6 us (0.942)
  Pallas kernels: 38.8 us -> 35.4 us
  local copies, waits for them, and re-layouts: 2.93 us -> 1.01 us
    pallas_call x2, Pallas kernels: 19 us -> 15.7 us  [the longest x1 9.9 us: synthesize(): pl.pallas_call(synthesis_kernel, in_specs=[whole, outside], out_specs=out...]
    unnamed x6 -> x2, local copies, waits for them, and re-layouts: 1.93 us -> 0.01 us
  transfers between devices with their start and end apart: 2 -> 2, of which waited for: 2 -> 2; matrix products, arithmetic and copies ran while one was open for 1% -> 1% of each run, Pallas kernels for 17% -> 18%
where the time goes in v2:
time: 88.6 us; the launch traced here: 88.3 us
  Pallas kernels  35.4 us (40%)
  waiting for transfers between devices  32 us (36%)
  starting transfers between devices  19.2 us (22%)
  local copies, waits for them, and re-layouts  1.01 us (1%)
    all_to_all x1, waiting for transfers between devices, on_device(): grid_spec = lax.all_to_all(grid_spec, 'lat', 0, 0, tiled=True)  31.1 us
    all_to_all x1, starting transfers between devices, on_device(): grid_spec = lax.all_to_all(grid_spec, 'lat', 0, 0, tiled=True)  12.6 us
    pallas_call x1, Pallas kernels, synthesize(): pl.pallas_call(synthesis_kernel, in_specs=[whole, outside], out_specs=out...  9.9 us
    pallas_call x1, Pallas kernels, fourier_table(): pl.pallas_call(fourier_kernel, grid=(4,), in_specs=[pl.BlockSpec((1, 1, L...  8.99 us
    pallas_call x1, Pallas kernels, legendre_table(): pl.pallas_call(table_kernel, grid=(M // CHUNK,), in_specs=[pl.BlockSpec(m...  6.98 us
    all_to_all x1, starting transfers between devices, exchanged(): return lax.all_to_all(spectra, 'scale', 0, 0, tiled=True)  6.64 us
    pallas_call x1, Pallas kernels, project(): pl.pallas_call(project_kernel, in_specs=[pl.BlockSpec(memory_space=pltpu....  5.76 us
    pallas_call x1, Pallas kernels, update(): pl.pallas_call(update_kernel, grid=(SLOTS // GROUP,), in_specs=[line, lin...  3.82 us
  transfers between devices with their start and end apart: 2, of which 2 were waited for; matrix products, arithmetic and copies ran while one was open for 1% of the time, Pallas kernels for 18%

profile of v2, /device:TPU:1, one launch (start us, length us, event | category | flops | bytes accessed | tf_op | source)
XLA Modules:
  0.0 88.3 jit_solution(2207726429338159678)
XLA Ops:
  0.6 0.0 copy-start
  0.6 3.8 %update.1 = (f32[8,2,128,128]{3,2,1,0:T(8,128)}, bf16[4,8,2,32,128]{4,3,2,1,0:T(8,128)(2,1)}) custom-call(f32[1,128]{1,0:T(1,128)} %bitcast.4, f32[1,128]{1,0:T(1,128)} %bitcast.5, f32[8,2,128,128]{3,2,1,0:T(8,128)} %state_ref.1, f32[8,2,128,128]{3,2,1,0:T(8,128)} %noise_ref.1), custom_call_target="tpu_custom_call" | custom-call | tf_op jit(solution)/shard_map/update/pallas_call | solution.py:88
  4.5 6.6 %all-to-all-start = ((bf16[4,8,2,32,128]{4,3,2,1,0:T(8,128)(2,1)}), bf16[4,8,2,32,128]{4,3,2,1,0:T(8,128)(2,1)S(1)}, u32[]{:S(2)}, u32[]{:S(2)}) async-start(bf16[4,8,2,32,128]{4,3,2,1,0:T(8,128)(2,1)} %get-tuple-element.5), calls=%async_computation | async-start | bytes 1048576 | tf_op jit(solution)/shard_map/all_to_all | solution.py:357
  11.1 7.0 %legendre.1.table_ref = bf16[8,512,768]{2,1,0:T(8,128)(2,1)} custom-call(s32[512]{0:T(512)} %orders_ref.3, f32[2,768]{1,0:T(2,128)} %constant.4.clone.lats_ref, f32[1,512]{1,0:T(1,128)} %constant.5.clone.head_ref), custom_call_target="tpu_custom_call" | custom-call | tf_op jit(solution)/shard_map/legendre/pallas_call | solution.py:161
  18.1 0.9 all-to-all-done.spectra_ref
  18.9 0.0 copy-done
  18.9 5.8 %project.1 = bf16[64,4,24,128]{3,2,1,0:T(8,128)(2,1)} custom-call(s32[512]{0:T(512)S(1)} %copy-done, bf16[4,8,2,32,128]{4,3,2,1,0:T(8,128)(2,1)S(1)} %all-to-all-done.spectra_ref, bf16[8,512,768]{2,1,0:T(8,128)(2,1)} %legendre.1.table_ref), custom_call_target="tpu_custom_call" | custom-call | tf_op jit(solution)/shard_map/project/pallas_call | solution.py:215
  24.7 12.6 %all-to-all-start.1 = ((bf16[64,4,24,128]{3,2,1,0:T(8,128)(2,1)}), bf16[64,4,24,128]{3,2,1,0:T(8,128)(2,1)S(1)}, u32[]{:S(2)}, u32[]{:S(2)}) async-start(bf16[64,4,24,128]{3,2,1,0:T(8,128)(2,1)} %project.1), calls=%async_computation.1 | async-start | bytes 3145728 | tf_op jit(solution)/shard_map/all_to_all | solution.py:367
  37.3 0.2 convert_element_type.10
  37.5 0.1 copy.9
  37.6 0.7 convert_element_type.12.orders_ref
  38.3 9.0 %fourier.1.fourier_ref = bf16[1024,3072]{1,0:T(8,128)(2,1)} custom-call(f32[4,1,128]{2,1,0:T(1,128)} %convert_element_type.12.orders_ref), custom_call_target="tpu_custom_call" | custom-call | tf_op jit(solution)/shard_map/fourier/pallas_call | solution.py:254
  47.3 31.1 %all-to-all-done.1.grid_ref = bf16[64,4,24,128]{3,2,1,0:T(8,128)(2,1)S(1)} async-done(((bf16[64,4,24,128]{3,2,1,0:T(8,128)(2,1)}), bf16[64,4,24,128]{3,2,1,0:T(8,128)(2,1)S(1)}, u32[]{:S(2)}, u32[]{:S(2)}) %all-to-all-start.1) | async-done | bytes 1572896 | tf_op jit(solution)/shard_map/all_to_all | solution.py:367
  78.4 9.9 %synthesis.1 = f32[32,24,3072]{2,1,0:T(8,128)} custom-call(bf16[64,4,24,128]{3,2,1,0:T(8,128)(2,1)S(1)} %all-to-all-done.1.grid_ref, bf16[1024,3072]{1,0:T(8,128)(2,1)} %fourier.1.fourier_ref), custom_call_target="tpu_custom_call" | custom-call | tf_op jit(solution)/shard_map/synthesis/pallas_call | solution.py:337
  (1 shorter events, 0.0 us)
Async XLA Ops:
  0.6 18.3 %copy-start = (s32[512]{0:T(512)S(1)}, s32[512]{0:T(512)}, u32[]{:S(2)}) copy-start(s32[512]{0:T(512)} %orders_ref.3) | copy-start | bytes 6148
  4.5 14.5 %all-to-all-start = ((bf16[4,8,2,32,128]{4,3,2,1,0:T(8,128)(2,1)}), bf16[4,8,2,32,128]{4,3,2,1,0:T(8,128)(2,1)S(1)}, u32[]{:S(2)}, u32[]{:S(2)}) async-start(bf16[4,8,2,32,128]{4,3,2,1,0:T(8,128)(2,1)} %get-tuple-element.5), calls=%async_computation | async-start | bytes 1048576 | tf_op jit(solution)/shard_map/all_to_all | solution.py:357
  24.7 53.7 %all-to-all-start.1 = ((bf16[64,4,24,128]{3,2,1,0:T(8,128)(2,1)}), bf16[64,4,24,128]{3,2,1,0:T(8,128)(2,1)S(1)}, u32[]{:S(2)}, u32[]{:S(2)}) async-start(bf16[64,4,24,128]{3,2,1,0:T(8,128)(2,1)} %project.1), calls=%async_computation.1 | async-start | bytes 3145728 | tf_op jit(solution)/shard_map/all_to_all | solution.py:367

commit v3 on v2

--- a/solution.py
+++ b/solution.py
@@ -22,10 +22,10 @@
 OWN_FIELDS = FIELDS // SCALE_PARTS
 PAIRS = SLOTS // 2
 CHUNK = 128
-GROUP = 2
+GROUP = 4
 WIDTH = 512
 PITCH = PAIRS * ROWS + 8
-BANDS = ((0, 8), (8, 16))
+BANDS = ((0, 8), (8, 8), (16, 8))
 
 log_floor = -60.0
 
@@ -56,7 +56,15 @@
     return head.astype(np.float32)[None]
 
 
-def update_kernel(time_ref, length_ref, state_ref, noise_ref, new_ref, spectra_ref, factor):
+def partner(scale, offset):
+    low = scale % 2
+    high = scale // 2
+    return (high + offset // 2) % 2 * 2 + (low + offset) % 2
+
+
+def update_kernel(time_ref, length_ref, state_ref, noise_ref, new_ref, *rest):
+    spectra_refs = rest[:SCALE_PARTS]
+    factor = rest[SCALE_PARTS]
     @pl.when(pl.program_id(0) == 0)
     def _():
         timescale = jnp.broadcast_to(time_ref[...], (FIELDS, FIELDS)).T
@@ -75,11 +83,12 @@
         for part in range(2):
             new = factor[0] * state_ref[slot, part] + factor[1] * noise_ref[slot, part]
             new_ref[slot, part] = new
-            rounded = new.astype(jnp.bfloat16)
-            for owner in range(SCALE_PARTS):
-                spectra_ref[owner, slot, part] = rounded[
-                    owner * OWN_FIELDS : (owner + 1) * OWN_FIELDS
-                ]
+            for offset in range(SCALE_PARTS):
+                owner = partner(lax.axis_index("scale"), offset)
+                first = pl.multiple_of(owner * OWN_FIELDS, OWN_FIELDS)
+                spectra_refs[offset][slot, part] = new_ref[
+                    slot, part, pl.ds(first, OWN_FIELDS), :
+                ].astype(jnp.bfloat16)
 
 
 def update(timescale, lengthscale, state, noise):
@@ -89,14 +98,10 @@
         update_kernel,
         grid=(SLOTS // GROUP,),
         in_specs=[line, line, block, block],
-        out_specs=[
-            block,
-            pl.BlockSpec((SCALE_PARTS, GROUP, 2, OWN_FIELDS, CHUNK), lambda s: (0, s, 0, 0, 0)),
-        ],
-        out_shape=[
-            jax.ShapeDtypeStruct((SLOTS, 2, FIELDS, CHUNK), jnp.float32),
-            jax.ShapeDtypeStruct((SCALE_PARTS, SLOTS, 2, OWN_FIELDS, CHUNK), jnp.bfloat16),
-        ],
+        out_specs=[block]
+        + [pl.BlockSpec((GROUP, 2, OWN_FIELDS, CHUNK), lambda s: (s, 0, 0, 0))] * SCALE_PARTS,
+        out_shape=[jax.ShapeDtypeStruct((SLOTS, 2, FIELDS, CHUNK), jnp.float32)]
+        + [jax.ShapeDtypeStruct((SLOTS, 2, OWN_FIELDS, CHUNK), jnp.bfloat16)] * SCALE_PARTS,
         scratch_shapes=[pltpu.VMEM((2, FIELDS, CHUNK), jnp.float32)],
         compiler_params=vmem_params(58, dimension_semantics=("arbitrary",)),
         name="update",
@@ -178,13 +183,23 @@
     )(orders, lats, head)
 
 
-def project_kernel(orders_ref, spectra_ref, table_ref, out_ref, table, arrived):
+def project_kernel(orders_ref, *rest):
+    spectra_refs = rest[:SCALE_PARTS]
+    table_ref, out_ref, table, arrived = rest[SCALE_PARTS:]
     lane = lax.broadcasted_iota(jnp.int32, (1, CHUNK), 1)
-    copies = [
-        pltpu.make_async_copy(table_ref.at[s], table.at[s], arrived.at[s]) for s in range(SLOTS)
-    ]
-    for copy in copies:
-        copy.start()
+    copies = []
+    for s in range(SLOTS):
+        for b in range(SCALE_PARTS):
+            block = partner(lax.axis_index("scale"), b)
+            first = pl.multiple_of(block * CHUNK, CHUNK)
+            copies.append(
+                pltpu.make_async_copy(
+                    table_ref.at[s, pl.ds(first, CHUNK)],
+                    table.at[s, pl.ds(b * CHUNK, CHUNK)],
+                    arrived.at[s, b],
+                )
+            )
+            copies[-1].start()
     for pair in range(PAIRS):
         north = []
         south = []
@@ -192,13 +207,15 @@
             order = orders_ref[lax.axis_index("lat") * SLOTS + 2 * pair + half]
             sign = (1 - 2 * ((lane + order) % 2)).astype(jnp.float32).astype(jnp.bfloat16)
             blocks = [
-                spectra_ref[b, 2 * pair + half].reshape(2 * OWN_FIELDS, CHUNK)
+                spectra_refs[b][2 * pair + half].reshape(2 * OWN_FIELDS, CHUNK)
                 for b in range(SCALE_PARTS)
             ]
             left = jnp.concatenate(
                 [jnp.concatenate([b, b * sign], axis=0) for b in blocks], axis=1
             )
-            copies[2 * pair + half].wait()
+            slot = 2 * pair + half
+            for copy in copies[slot * SCALE_PARTS : (slot + 1) * SCALE_PARTS]:
+                copy.wait()
             product = jnp.dot(left, table[2 * pair + half], preferred_element_type=jnp.float32)
             north.append(product[: 2 * OWN_FIELDS])
             south.append(product[2 * OWN_FIELDS :])
@@ -214,16 +231,16 @@
 def project(orders, spectra, table):
     return pl.pallas_call(
         project_kernel,
-        in_specs=[pl.BlockSpec(memory_space=pltpu.SMEM), whole, outside],
+        in_specs=[pl.BlockSpec(memory_space=pltpu.SMEM)] + [whole] * SCALE_PARTS + [outside],
         out_specs=whole,
         out_shape=jax.ShapeDtypeStruct((LAT_PARTS, PAIRS, ROWS, LANES), jnp.bfloat16),
         scratch_shapes=[
             pltpu.VMEM((SLOTS, M, HALF), jnp.bfloat16),
-            pltpu.SemaphoreType.DMA((SLOTS,)),
+            pltpu.SemaphoreType.DMA((SLOTS, SCALE_PARTS)),
         ],
         compiler_params=vmem_params(52),
         name="project",
-    )(orders, spectra, table)
+    )(orders, *spectra, table)
 
 
 def remainder(value, divisor):
@@ -354,13 +371,17 @@
 
 
 def exchanged(spectra):
-    return lax.all_to_all(spectra, "scale", 0, 0, tiled=True)
+    received = [spectra[0]]
+    for offset in range(1, SCALE_PARTS):
+        pairs = [(k, partner(k, offset)) for k in range(SCALE_PARTS)]
+        received.append(lax.ppermute(spectra[offset], "scale", pairs))
+    return received
 
 
 def on_device(state, noise, slot_wavenumber, timescale, lengthscale):
     lats = jnp.asarray(latitude_constants())
     head = jnp.asarray(log_head_table())
-    new_state, spectra = update(timescale[None], lengthscale[None], state, noise)
+    new_state, *spectra = update(timescale[None], lengthscale[None], state, noise)
     spectra = exchanged(spectra)
     table = legendre_table(slot_wavenumber, lats, head)
     grid_spec = project(slot_wavenumber, spectra, table)

time: 88.6 us -> 85 us (0.959)
  Pallas kernels: 35.4 us -> 33.6 us
  starting transfers between devices: 19.2 us -> 17.8 us
  waiting for transfers between devices: 32 us -> 30.9 us
    all_to_all x1 -> x0, starting transfers between devices: 6.64 us -> none  [exchanged(): return lax.all_to_all(spectra, 'scale', 0, 0, tiled=True)]
    ppermute x0 -> x3, starting transfers between devices: none -> 5.01 us  [exchanged(): received.append(lax.ppermute(spectra[offset], 'scale', pairs))]
    pallas_call x1, Pallas kernels: 3.82 us -> 2.62 us  [update(): pl.pallas_call(update_kernel, grid=(SLOTS // GROUP,), in_specs=[line, lin...]
    pallas_call x1, Pallas kernels: 9.9 us -> 8.94 us  [synthesize(): pl.pallas_call(synthesis_kernel, in_specs=[whole, outside], out_specs=out...]
  transfers between devices with their start and end apart: 2 -> 4, of which waited for: 2 -> 1; matrix products, arithmetic and copies ran while one was open for 1% -> 1% of each run, Pallas kernels for 18% -> 19%
where the time goes in v3:
time: 85 us; the launch traced here: 84.2 us
  Pallas kernels  33.6 us (40%)
  waiting for transfers between devices  30.9 us (36%)
  starting transfers between devices  17.8 us (21%)
  local copies, waits for them, and re-layouts  1.01 us (1%)
  between operations  0.86 us (1%)
    all_to_all x1, waiting for transfers between devices, on_device(): grid_spec = lax.all_to_all(grid_spec, 'lat', 0, 0, tiled=True)  30.9 us
    all_to_all x1, starting transfers between devices, on_device(): grid_spec = lax.all_to_all(grid_spec, 'lat', 0, 0, tiled=True)  12.8 us
    pallas_call x1, Pallas kernels, fourier_table(): pl.pallas_call(fourier_kernel, grid=(4,), in_specs=[pl.BlockSpec((1, 1, L...  9 us
    pallas_call x1, Pallas kernels, synthesize(): pl.pallas_call(synthesis_kernel, in_specs=[whole, outside], out_specs=out...  8.94 us
    pallas_call x1, Pallas kernels, legendre_table(): pl.pallas_call(table_kernel, grid=(M // CHUNK,), in_specs=[pl.BlockSpec(m...  6.98 us
    pallas_call x1, Pallas kernels, project(): pl.pallas_call(project_kernel, in_specs=[pl.BlockSpec(memory_space=pltpu....  6.1 us
    ppermute x3, starting transfers between devices, exchanged(): received.append(lax.ppermute(spectra[offset], 'scale', pairs))  5.01 us
    pallas_call x1, Pallas kernels, update(): pl.pallas_call(update_kernel, grid=(SLOTS // GROUP,), in_specs=[line, lin...  2.62 us
  transfers between devices with their start and end apart: 4, of which 1 were waited for; matrix products, arithmetic and copies ran while one was open for 1% of the time, Pallas kernels for 19%

profile of v3, /device:TPU:1, one launch (start us, length us, event | category | flops | bytes accessed | tf_op | source)
XLA Modules:
  0.0 84.2 jit_solution(12180419018851000825)
XLA Ops:
  0.6 0.0 copy-start.1
  0.6 2.6 %update.1 = (f32[8,2,128,128]{3,2,1,0:T(8,128)}, bf16[8,2,32,128]{3,2,1,0:T(8,128)(2,1)}, bf16[8,2,32,128]{3,2,1,0:T(8,128)(2,1)}, bf16[8,2,32,128]{3,2,1,0:T(8,128)(2,1)}, bf16[8,2,32,128]{3,2,1,0:T(8,128)(2,1)}) custom-call(f32[1,128]{1,0:T(1,128)} %bitcast.4, f32[1,128]{1,0:T(1,128)} %bitcast.5, f32[8,2,128,128]{3,2,1,0:T(8,128)} %state_ref.1, ...), custom_call_target="tpu_custom_call" | custom-call | tf_op jit(solution)/shard_map/update/pallas_call | solution.py:97
  3.3 0.0 copy-start
  3.3 3.3 %collective-permute-start = (bf16[8,2,32,128]{3,2,1,0:T(8,128)(2,1)}, bf16[8,2,32,128]{3,2,1,0:T(8,128)(2,1)S(1)}, u32[]{:S(2)}, u32[]{:S(2)}) collective-permute-start(bf16[8,2,32,128]{3,2,1,0:T(8,128)(2,1)} %get-tuple-element.9), channel_id=1, source_target_pairs={{0,1},{1,0},{2,3},{3,2},{4,5},{5,4},{6,7},{7,6},{8,9},{9,8},{10,11... | collective-permute-start | bytes 393224 | tf_op jit(solution)/shard_map/ppermute | solution.py:377
  6.5 0.0 collective-permute-start.1
  6.5 1.7 %collective-permute-start.2 = (bf16[8,2,32,128]{3,2,1,0:T(8,128)(2,1)}, bf16[8,2,32,128]{3,2,1,0:T(8,128)(2,1)S(1)}, u32[]{:S(2)}, u32[]{:S(2)}) collective-permute-start(bf16[8,2,32,128]{3,2,1,0:T(8,128)(2,1)} %get-tuple-element.11), channel_id=1, source_target_pairs={{0,3},{1,2},{2,1},{3,0},{4,7},{5,6},{6,5},{7,4},{8,11},{9,10},{10,... | collective-permute-start | bytes 393224 | tf_op jit(solution)/shard_map/ppermute | solution.py:377
  8.3 7.0 %legendre.1.rest_4_ = bf16[8,512,768]{2,1,0:T(8,128)(2,1)} custom-call(s32[512]{0:T(512)} %orders_ref.3, f32[2,768]{1,0:T(2,128)} %constant.4.clone.lats_ref, f32[1,512]{1,0:T(1,128)} %constant.5.clone.head_ref), custom_call_target="tpu_custom_call" | custom-call | tf_op jit(solution)/shard_map/legendre/pallas_call | solution.py:166
  15.3 0.0 collective-permute-done.rest_1_
  15.3 0.0 collective-permute-done.1.rest_2_
  15.3 0.0 collective-permute-done.2.rest_3_
  15.3 0.0 copy-done.1
  15.3 0.0 copy-done
  15.3 6.1 %project.1 = bf16[64,4,24,128]{3,2,1,0:T(8,128)(2,1)} custom-call(s32[512]{0:T(512)S(1)} %copy-done.1, bf16[8,2,32,128]{3,2,1,0:T(8,128)(2,1)S(1)} %copy-done, bf16[8,2,32,128]{3,2,1,0:T(8,128)(2,1)S(1)} %collective-permute-done.rest_1_, bf16[8,2,32,128]{3,2,1,0:T(8,128)(2,1)S(1)} %collective-permute-done.1.rest_2_, ...), custom_call_target="tpu_custom_call" | custom-call | tf_op jit(solution)/shard_map/project/pallas_call | solution.py:232
  21.4 12.8 %all-to-all-start = ((bf16[64,4,24,128]{3,2,1,0:T(8,128)(2,1)}), bf16[64,4,24,128]{3,2,1,0:T(8,128)(2,1)S(1)}, u32[]{:S(2)}, u32[]{:S(2)}) async-start(bf16[64,4,24,128]{3,2,1,0:T(8,128)(2,1)} %project.1), calls=%async_computation | async-start | bytes 3145728 | tf_op jit(solution)/shard_map/all_to_all | solution.py:388
  34.2 0.2 convert_element_type.10
  34.4 0.1 copy.9
  34.5 0.7 convert_element_type.12.orders_ref
  35.2 9.0 %fourier.1.fourier_ref = bf16[1024,3072]{1,0:T(8,128)(2,1)} custom-call(f32[4,1,128]{2,1,0:T(1,128)} %convert_element_type.12.orders_ref), custom_call_target="tpu_custom_call" | custom-call | tf_op jit(solution)/shard_map/fourier/pallas_call | solution.py:271
  44.2 30.9 %all-to-all-done.grid_ref = bf16[64,4,24,128]{3,2,1,0:T(8,128)(2,1)S(1)} async-done(((bf16[64,4,24,128]{3,2,1,0:T(8,128)(2,1)}), bf16[64,4,24,128]{3,2,1,0:T(8,128)(2,1)S(1)}, u32[]{:S(2)}, u32[]{:S(2)}) %all-to-all-start) | async-done | bytes 1572896 | tf_op jit(solution)/shard_map/all_to_all | solution.py:388
  75.1 8.9 %synthesis.1 = f32[32,24,3072]{2,1,0:T(8,128)} custom-call(bf16[64,4,24,128]{3,2,1,0:T(8,128)(2,1)S(1)} %all-to-all-done.grid_ref, bf16[1024,3072]{1,0:T(8,128)(2,1)} %fourier.1.fourier_ref), custom_call_target="tpu_custom_call" | custom-call | tf_op jit(solution)/shard_map/synthesis/pallas_call | solution.py:354
  (1 shorter events, 0.0 us)
Async XLA Ops:
  0.6 14.6 %copy-start.1 = (s32[512]{0:T(512)S(1)}, s32[512]{0:T(512)}, u32[]{:S(2)}) copy-start(s32[512]{0:T(512)} %orders_ref.3) | copy-start | bytes 6148
  3.3 12.0 %copy-start = (bf16[8,2,32,128]{3,2,1,0:T(8,128)(2,1)S(1)}, bf16[8,2,32,128]{3,2,1,0:T(8,128)(2,1)}, u32[]{:S(2)}) copy-start(bf16[8,2,32,128]{3,2,1,0:T(8,128)(2,1)} %get-tuple-element.8.rest_0_) | copy-start | bytes 393220
  3.3 12.0 %collective-permute-start = (bf16[8,2,32,128]{3,2,1,0:T(8,128)(2,1)}, bf16[8,2,32,128]{3,2,1,0:T(8,128)(2,1)S(1)}, u32[]{:S(2)}, u32[]{:S(2)}) collective-permute-start(bf16[8,2,32,128]{3,2,1,0:T(8,128)(2,1)} %get-tuple-element.9), channel_id=1, source_target_pairs={{0,1},{1,0},{2,3},{3,2},{4,5},{5,4},{6,7},{7,6},{8,9},{9,8},{10,11... | collective-permute-start | bytes 393224 | tf_op jit(solution)/shard_map/ppermute | solution.py:377
  6.5 8.7 %collective-permute-start.1 = (bf16[8,2,32,128]{3,2,1,0:T(8,128)(2,1)}, bf16[8,2,32,128]{3,2,1,0:T(8,128)(2,1)S(1)}, u32[]{:S(2)}, u32[]{:S(2)}) collective-permute-start(bf16[8,2,32,128]{3,2,1,0:T(8,128)(2,1)} %get-tuple-element.10), channel_id=1, source_target_pairs={{0,2},{1,3},{2,0},{3,1},{4,6},{5,7},{6,4},{7,5},{8,10},{9,11},{10,... | collective-permute-start | bytes 393224 | tf_op jit(solution)/shard_map/ppermute | solution.py:377
  6.5 8.7 %collective-permute-start.2 = (bf16[8,2,32,128]{3,2,1,0:T(8,128)(2,1)}, bf16[8,2,32,128]{3,2,1,0:T(8,128)(2,1)S(1)}, u32[]{:S(2)}, u32[]{:S(2)}) collective-permute-start(bf16[8,2,32,128]{3,2,1,0:T(8,128)(2,1)} %get-tuple-element.11), channel_id=1, source_target_pairs={{0,3},{1,2},{2,1},{3,0},{4,7},{5,6},{6,5},{7,4},{8,11},{9,10},{10,... | collective-permute-start | bytes 393224 | tf_op jit(solution)/shard_map/ppermute | solution.py:377
  21.4 53.7 %all-to-all-start = ((bf16[64,4,24,128]{3,2,1,0:T(8,128)(2,1)}), bf16[64,4,24,128]{3,2,1,0:T(8,128)(2,1)S(1)}, u32[]{:S(2)}, u32[]{:S(2)}) async-start(bf16[64,4,24,128]{3,2,1,0:T(8,128)(2,1)} %project.1), calls=%async_computation | async-start | bytes 3145728 | tf_op jit(solution)/shard_map/all_to_all | solution.py:388
